TPU v7x, 32 devices: a whole 2x2x4 slice. The times are simulated.
32 devices in a mesh: member: 2 (over y), gy: 4 (over z), gx: 2 (over x), lev: 2 (over core).
Axes of the slice: x: 2, y: 2, z: 4, core: 2. Of those that a mesh axis runs over, the one named last changes fastest.
Arguments:
- level_field: bfloat16 [32, 1536, 1536], P(('member', 'lev'), 'gy', 'gx'), parts along dimension 0, may hold values from -6 to 6
Outputs:
- spectra: float32 [1536, 32, 1536], P(('gy', 'gx'), ('member', 'lev')), parts along dimension 1
- spectra_zone: float32 [1536, 32, 11], P(('gy', 'gx'), ('member', 'lev')), parts along dimension 1
There are 2 independent parts, one for each index of `member`. A program takes and returns all parts, laid end to end along the dimension named above; each array names one. Nothing has to cross between parts.
All inputs are finite; a program needn't handle non-finite values.
Results may differ from a plain program's by a relative error of at most 0.0042.
Values may be sent and summed in bfloat16 or wider, within the bound.
A program may use at most 128 MiB of HBM per device.

v0:
```python
import functools
import math

import jax
import jax.numpy as jnp
from jax import lax
from jax.experimental import pallas as pl
from jax.experimental.pallas import tpu as pltpu
from jax.sharding import PartitionSpec as P

EXT_ZONE = 11
LANES = 128
NT = (((1,), (1,)), ((), ()))
MESH = pl.DeviceIdType.MESH


def blend_weights(zone_count):
    steps = (jnp.arange(zone_count, dtype=jnp.int32) + 1).astype(jnp.float32) / (zone_count + 1.0)
    weight_a = 2.0 * steps**3 - 3.0 * steps**2 + 1.0
    weight_b = steps**3 - 2.0 * steps**2 + steps
    weight_c = -2.0 * steps**3 + 3.0 * steps**2
    weight_d = steps**3 - steps**2
    return weight_a, weight_b, weight_c, weight_d


def blend_zone(second_last, last_value, first_value, second_value, zone_count):
    weight_a, weight_b, weight_c, weight_d = blend_weights(zone_count)
    tangent_scale = zone_count + 1.0
    slope_start = tangent_scale * (last_value - second_last)
    slope_end = tangent_scale * (second_value - first_value)
    return (
        last_value[..., None] * weight_a
        + slope_start[..., None] * weight_b
        + first_value[..., None] * weight_c
        + slope_end[..., None] * weight_d
    )


def wave_factors(coeff0, group, column, wave_count, length):
    number0 = jnp.where(coeff0 < wave_count, coeff0, coeff0 - wave_count + 1)
    scale = 2.0 * math.pi / length
    phase0 = (number0[:, None] * column[None, :] % length).astype(jnp.float32) * scale
    cos0, sin0 = jnp.cos(phase0), jnp.sin(phase0)
    is_cosine = (coeff0 < wave_count)[:, None]
    p, q = jnp.where(is_cosine, cos0, -sin0), jnp.where(is_cosine, sin0, cos0)
    step = jnp.arange(group, dtype=jnp.int32)
    phase = (step[:, None] * column[None, :] % length).astype(jnp.float32) * scale
    norm = 1.0 / math.sqrt(length)
    return p, q, jnp.cos(phase) * norm, jnp.sin(phase) * norm


def kernel(n_gx, n_gy, field_ref, edge_ref, table_ref, ztable_ref, weight_ref,
           out_ref, out_edge_ref, xgot, xedge, send, esend, xs, xr, es, er, zs, zr, ts, tr):
    levels, rows, cols = field_ref.shape
    bands = table_ref.shape[2]
    me_x, me_y = lax.axis_index("gx"), lax.axis_index("gy")

    def peer_x(shift):
        return {"gx": lax.rem(me_x + n_gx - shift, n_gx)}

    def peer_y(shift):
        return {"gy": lax.rem(me_y + shift, n_gy)}

    barrier = pltpu.get_barrier_semaphore()
    for shift in range(1, n_gx):
        pl.semaphore_signal(barrier, inc=1, device_id=peer_x(shift), device_id_type=MESH)
    for shift in range(1, n_gy):
        pl.semaphore_signal(barrier, inc=1, device_id=peer_y(shift), device_id_type=MESH)
    pl.semaphore_wait(barrier, n_gx + n_gy - 2)

    def edge_x(shift):
        return pltpu.make_async_remote_copy(
            src_ref=edge_ref, dst_ref=xedge.at[shift - 1], send_sem=es.at[shift - 1],
            recv_sem=er.at[shift - 1], device_id=peer_x(shift), device_id_type=MESH)

    def rows_x(shift, level):
        return pltpu.make_async_remote_copy(
            src_ref=field_ref.at[level], dst_ref=xgot.at[shift - 1, level],
            send_sem=xs.at[shift - 1, level], recv_sem=xr.at[shift - 1, level],
            device_id=peer_x(shift), device_id_type=MESH)

    def edge_y(shift):
        return pltpu.make_async_remote_copy(
            src_ref=esend.at[shift - 1], dst_ref=out_edge_ref.at[shift], send_sem=ts.at[shift - 1],
            recv_sem=tr.at[shift - 1], device_id=peer_y(shift), device_id_type=MESH)

    def spec_y(shift, level):
        return pltpu.make_async_remote_copy(
            src_ref=send.at[shift - 1, level], dst_ref=out_ref.at[shift, level],
            send_sem=zs.at[shift - 1, level], recv_sem=zr.at[shift - 1, level],
            device_id=peer_y(shift), device_id_type=MESH)

    for shift in range(1, n_gx):
        edge_x(shift).start()

    @pl.loop(0, levels)
    def _(level):
        for shift in range(1, n_gx):
            rows_x(shift, level).start()

    tail = (cols - 1) // LANES * LANES

    def zone_of(parts):
        first = second = last = before = 0.0
        for at, part in enumerate(parts):
            owner = lax.rem(me_x + at, n_gx)
            is_first = jnp.where(owner == 0, 1.0, 0.0)
            is_last = jnp.where(owner == n_gx - 1, 1.0, 0.0)
            head = part[:, :min(LANES, cols)].astype(jnp.float32)
            rear = part[:, tail:].astype(jnp.float32)
            first += is_first * head[:, 0:1]
            second += is_first * head[:, 1:2]
            before += is_last * rear[:, cols - 2 - tail:cols - 1 - tail]
            last += is_last * rear[:, cols - 1 - tail:cols - tail]
        tangent = EXT_ZONE + 1.0
        zone = (last * weight_ref[0:1, :] + (tangent * (last - before)) * weight_ref[1:2, :]
                + first * weight_ref[2:3, :] + (tangent * (second - first)) * weight_ref[3:4, :])
        return zone.astype(jnp.bfloat16)

    def dot(a, b):
        return lax.dot_general(a, b, NT, preferred_element_type=jnp.float32)

    for shift in range(1, n_gx):
        edge_x(shift).wait_recv()
    parts = [edge_ref[...]] + [xedge[at] for at in range(n_gx - 1)]
    zone = zone_of(parts)
    for shift in range(n_gy):
        total = dot(zone, ztable_ref[shift])
        for at, part in enumerate(parts):
            total += dot(part, table_ref[at, shift])
        if shift == 0:
            out_edge_ref[0] = total
        else:
            esend[shift - 1] = total
            edge_y(shift).start()

    merged = bands % 16 == 0

    @pl.loop(0, levels)
    def _(level):
        for shift in range(1, n_gx):
            rows_x(shift, level).wait_recv()
        parts = [field_ref[level]] + [xgot[at, level] for at in range(n_gx - 1)]
        zone = zone_of(parts)
        if merged:
            size = n_gy * bands
            total = dot(ztable_ref[...].reshape(size, LANES), zone)
            for at, part in enumerate(parts):
                total += dot(table_ref[at].reshape(size, cols), part)
            pieces = [total[s * bands:(s + 1) * bands] for s in range(n_gy)]
        else:
            pieces = []
            for shift in range(n_gy):
                total = dot(ztable_ref[shift], zone)
                for at, part in enumerate(parts):
                    total += dot(table_ref[at, shift], part)
                pieces.append(total)
        for shift in range(n_gy):
            piece = pieces[shift].astype(jnp.bfloat16)
            if shift == 0:
                out_ref[0, level] = piece
            else:
                send[shift - 1, level] = piece
        for shift in range(1, n_gy):
            spec_y(shift, level).start()

    for shift in range(1, n_gx):
        edge_x(shift).wait_send()
    for shift in range(1, n_gy):
        edge_y(shift).wait()

    @pl.loop(0, levels)
    def _(level):
        for shift in range(1, n_gx):
            rows_x(shift, level).wait_send()
        for shift in range(1, n_gy):
            spec_y(shift, level).wait()


def make_body(mesh):
    n_gx, n_gy = mesh.shape["gx"], mesh.shape["gy"]

    def body(field):
        levels, rows, cols = field.shape
        nx, ny = cols * n_gx, rows * n_gy
        length = nx + EXT_ZONE
        me_x, me_y = lax.axis_index("gx"), lax.axis_index("gy")
        bands = nx // (n_gx * n_gy)
        assert (nx // 2) % bands == 0
        group = 16 if bands % 16 == 0 else bands

        at = jnp.arange(nx + LANES, dtype=jnp.int32)
        column = jnp.where(at < nx, (at + me_x * cols) % nx, at)
        shift_at = jnp.arange(n_gy, dtype=jnp.int32)[:, None]
        coeff = ((me_y + shift_at) % n_gy) * (n_gx * bands) + me_x * bands
        coeff = (coeff + jnp.arange(0, bands, group, dtype=jnp.int32)[None, :]).reshape(-1)
        factors = wave_factors(coeff, group, column, nx // 2, length)
        p, q, c, s = lax.optimization_barrier(factors)

        def expand(lo, hi):
            full = p[:, None, lo:hi] * c[None, :, lo:hi] - q[:, None, lo:hi] * s[None, :, lo:hi]
            return full.astype(jnp.bfloat16).reshape(n_gy, bands, hi - lo)

        table = jnp.stack([expand(i * cols, (i + 1) * cols) for i in range(n_gx)])
        ztable = expand(nx, nx + LANES)
        ztable = jnp.where(jnp.arange(LANES) < EXT_ZONE, ztable, jnp.zeros_like(ztable))
        weights = jnp.pad(jnp.stack(blend_weights(EXT_ZONE)), ((0, 4), (0, LANES - EXT_ZONE)))
        edge = jnp.concatenate([field[:, :2], field[:, rows - 2:]], axis=1)
        edge = edge.transpose(1, 0, 2).reshape(4 * levels, cols)

        vmem = pl.BlockSpec(memory_space=pltpu.VMEM)
        dma = pltpu.SemaphoreType.DMA
        xs, ys = n_gx - 1, n_gy - 1
        got, edge_got = pl.pallas_call(
            functools.partial(kernel, n_gx, n_gy),
            out_shape=(
                jax.ShapeDtypeStruct((n_gy, levels, bands, rows), jnp.bfloat16),
                jax.ShapeDtypeStruct((n_gy, 4 * levels, bands), jnp.float32),
            ),
            in_specs=[vmem] * 5,
            out_specs=(vmem, vmem),
            scratch_shapes=[
                pltpu.VMEM((xs, levels, rows, cols), jnp.bfloat16),
                pltpu.VMEM((xs, 4 * levels, cols), jnp.bfloat16),
                pltpu.VMEM((ys, levels, bands, rows), jnp.bfloat16),
                pltpu.VMEM((ys, 4 * levels, bands), jnp.float32),
                dma((xs, levels)), dma((xs, levels)), dma((xs,)), dma((xs,)),
                dma((ys, levels)), dma((ys, levels)), dma((ys,)), dma((ys,)),
            ],
            compiler_params=pltpu.CompilerParams(collective_id=0, has_side_effects=True),
        )(field, edge, table, ztable, weights)

        edge_got = edge_got.reshape(n_gy, 4, levels, bands)
        low = lax.dynamic_index_in_dim(edge_got, me_y, 0, keepdims=False)
        high = lax.dynamic_index_in_dim(edge_got, (me_y + 1) % n_gy, 0, keepdims=False)
        low, high = low.transpose(0, 2, 1), high.transpose(0, 2, 1)
        spectra_zone = blend_zone(high[2], high[3], low[0], low[1], EXT_ZONE)

        spectra = jnp.zeros((bands, levels, ny), jnp.float32)
        for shift in range(n_gy):
            full = got[shift].transpose(1, 0, 2).astype(jnp.float32)
            source = (me_y + n_gy - shift) % n_gy
            spectra = lax.dynamic_update_slice(spectra, full, (0, 0, source * rows))
        return spectra, spectra_zone

    return body


def solution(mesh):
    return jax.shard_map(
        make_body(mesh),
        mesh=mesh,
        in_specs=(P(("member", "lev"), "gy", "gx"),),
        out_specs=(
            P(("gy", "gx"), ("member", "lev"), None),
            P(("gy", "gx"), ("member", "lev"), None),
        ),
        check_vma=False,
    )
```

profile of v0, /device:TPU:0, one launch (start us, length us, event | category | flops | bytes accessed | tf_op | source)
XLA Modules:
  0.0 161.1 jit_solution(4292737103615597285)
XLA Ops:
  0.7 0.1 broadcast_add_fusion
  0.7 0.1 add.270
  0.9 1.4 fusion.6
  2.3 0.5 sine_multiply_fusion
  2.7 0.1 fusion.31
  2.8 0.5 subtract_convert_fusion.1
  3.3 0.5 subtract_convert_fusion
  3.7 1.6 pad_maximum_fusion.table_ref
  5.4 0.1 subtract_convert_fusion.2
  5.4 0.7 bitcast_select_fusion.ztable_ref
  6.2 0.6 select_maximum_fusion.weight_ref
  6.8 1.0 fusion.30
  7.8 0.1 maximum_bitcast_fusion
  7.8 0.6 copy.13
  8.4 126.8 %shard_map.30 = (bf16[4,8,192,384]{3,2,1,0:T(8,128)(2,1)}, f32[4,32,192]{2,1,0:T(8,128)}) custom-call(bf16[8,384,768]{2,1,0:T(8,128)(2,1)} %field_ref.1, bf16[32,768]{1,0:T(8,128)(2,1)} %bitcast.62, bf16[2,4,192,768]{3,2,1,0:T(8,128)(2,1)} %pad_maximum_fusion.table_ref, bf16[4,192,128]{2,1,0:T(8,128)(2,1)} %bitcast_select_fusion.ztable_ref, ...), custom_call_target="tpu_custom_call" | custom-call | tf_op jit(solution)/shard_map/pallas_call | solution.py:214
  135.3 0.8 dynamic-slice_bitcast_fusion.1
  136.1 0.8 multiply_add_fusion
  136.9 5.5 %convert_bitcast_fusion = (f32[192,8,384]{2,0,1:T(8,128)S(1)}, f32[192,8,384]{2,0,1:T(8,128)}, f32[192,8,384]{2,0,1:T(8,128)}, f32[192,8,384]{2,0,1:T(8,128)}) fusion(bf16[4,8,192,384]{3,2,1,0:T(8,128)(2,1)} %get-tuple-element.12), kind=kLoop, calls=%fused_computation.1 | loop fusion | flops 2359296 | bytes 14155776 | tf_op jit(solution)/shard_map/convert_element_type | solution.py:241
  142.4 0.0 copy-start
  142.4 1.2 broadcast_in_dim.18
  143.6 0.5 copy-done
  144.1 1.6 copy_dynamic-update-slice_fusion.3
  145.7 0.0 copy-start.1
  145.7 3.7 %copy-done.1 = f32[192,8,1536]{2,1,0:T(8,128)} copy-done((f32[192,8,1536]{2,1,0:T(8,128)}, f32[192,8,1536]{2,1,0:T(8,128)S(1)}, u32[]{:S(2)}) %copy-start.1) | copy-done | bytes 9437208
  149.4 4.4 %copy_dynamic-update-slice_fusion.2 = f32[192,8,1536]{2,1,0:T(8,128)} fusion(f32[192,8,1536]{2,1,0:T(8,128)} %copy-done.1, s32[]{:T(128)S(6)} %select_n.112, f32[192,8,384]{2,0,1:T(8,128)} %get-tuple-element.16), kind=kLoop, calls=%fused_computation.7 | loop fusion | bytes 4718596 | tf_op jit(solution)/shard_map/dynamic_update_slice | solution.py:243
  153.9 4.4 %copy_dynamic-update-slice_fusion.1 = f32[192,8,1536]{2,1,0:T(8,128)} fusion(f32[192,8,1536]{2,1,0:T(8,128)} %copy_dynamic-update-slice_fusion.2, s32[]{:T(128)S(6)} %select_n.114, f32[192,8,384]{2,0,1:T(8,128)} %get-tuple-element.15), kind=kLoop, calls=%fused_computation.6 | loop fusion | bytes 4718596 | tf_op jit(solution)/shard_map/dynamic_update_slice | solution.py:243
  158.3 2.8 %copy_dynamic-update-slice_fusion = f32[192,8,1536]{2,1,0:T(8,128)} fusion(f32[192,8,1536]{2,1,0:T(8,128)} %copy_dynamic-update-slice_fusion.1, s32[]{:T(128)S(6)} %select_n.116, f32[192,8,384]{2,0,1:T(8,128)S(1)} %get-tuple-element.14), kind=kLoop, calls=%fused_computation.5 | loop fusion | bytes 4718596 | tf_op jit(solution)/shard_map/dynamic_update_slice | solution.py:243
  (19 shorter events, 0.1 us)
Async XLA Ops:
  142.4 1.7 %copy-start = (f32[192,8,384]{2,0,1:T(8,128)S(1)}, f32[192,8,384]{2,0,1:T(8,128)}, u32[]{:S(2)}) copy-start(f32[192,8,384]{2,0,1:T(8,128)} %get-tuple-element.17) | copy-start | bytes 7077892
  145.7 3.7 %copy-start.1 = (f32[192,8,1536]{2,1,0:T(8,128)}, f32[192,8,1536]{2,1,0:T(8,128)S(1)}, u32[]{:S(2)}) copy-start(f32[192,8,1536]{2,1,0:T(8,128)S(1)} %copy_dynamic-update-slice_fusion.3) | copy-start | bytes 28311556
where the time goes:
time: 162 us; the launch traced here: 161 us
  Pallas kernels  127 us (78%)
  local copies, waits for them, and re-layouts  21.2 us (13%)
  other arithmetic  12.3 us (8%)
    pallas_call x1, Pallas kernels, body(): pl.pallas_call(functools.partial(kernel, n_gx, n_gy), out_shape=(jax.Shap...  127 us
    dynamic_update_slice x4, local copies, waits for them, and re-layouts, body(): spectra = lax.dynamic_update_slice(spectra, full, (0, 0, source * rows))  13.2 us
    convert_element_type x1, other arithmetic, body(): full = got[shift].transpose(1, 0, 2).astype(jnp.float32)  5.52 us
    unnamed x4, local copies, waits for them, and re-layouts  4.22 us

commit v1 on v0

--- a/solution.py
+++ b/solution.py
@@ -3,6 +3,7 @@
 
 import jax
 import jax.numpy as jnp
+import numpy as np
 from jax import lax
 from jax.experimental import pallas as pl
 from jax.experimental.pallas import tpu as pltpu
@@ -177,7 +178,7 @@
             spec_y(shift, level).wait()
 
 
-def make_body(mesh):
+def make_plain_body(mesh):
     n_gx, n_gy = mesh.shape["gx"], mesh.shape["gy"]
 
     def body(field):
@@ -246,14 +247,366 @@
     return body
 
 
+ROWS = 128
+GROUP = 16
+
+
+def host_weights(zone_count):
+    t = (np.arange(zone_count, dtype=np.float32) + np.float32(1)) / np.float32(zone_count + 1.0)
+    two, three, one = np.float32(2), np.float32(3), np.float32(1)
+    cube, square = t * t * t, t * t
+    return (two * cube - three * square + one, cube - two * square + t,
+            three * square - two * cube, cube - square)
+
+
+def unit_circle(product, length):
+    quarter = length / 4.0
+    turns = jnp.floor(product * (4.0 / length) + 0.5)
+    theta = (product - turns * quarter) * (2.0 * math.pi / length)
+    turns = turns - 4.0 * jnp.floor(turns * 0.25)
+    z = theta * theta
+    sin = theta * (1.0 + z * (-1.0 / 6 + z * (1.0 / 120 + z * (-1.0 / 5040 + z * (1.0 / 362880)))))
+    cos = 1.0 + z * (-0.5 + z * (1.0 / 24 + z * (-1.0 / 720 + z * (1.0 / 40320 - z * (1.0 / 3628800)))))
+    odd = (turns == 1.0) | (turns == 3.0)
+    c, s = jnp.where(odd, sin, cos), jnp.where(odd, cos, sin)
+    c = jnp.where((turns == 1.0) | (turns == 2.0), -c, c)
+    s = jnp.where(turns >= 2.0, -s, s)
+    return c, s
+
+
+def fused_kernel(n_gx, n_gy, field_ref, out_ref, zone_ref,
+                 own, xgot, got, send, tab, ztab, pq, cs, acc, esum, esend, egot,
+                 ls, xs, xr, zs, zr, fs, fr, *, depth, lag):
+    levels, rows, cols = field_ref.shape
+    bands = got.shape[3]
+    nblk = rows // ROWS
+    size = n_gy * bands
+    nx = n_gx * cols
+    length = nx + EXT_ZONE
+    me_x, me_y = lax.axis_index("gx"), lax.axis_index("gy")
+    chunks = levels * nblk
+    order = sorted(range(1, n_gy), key=lambda shift: abs(2 * shift - n_gy))
+
+    def peer_x(shift):
+        return {"gx": lax.rem(me_x + n_gx - shift, n_gx)}
+
+    def peer_y(shift):
+        return {"gy": lax.rem(me_y + shift, n_gy)}
+
+    def source_y(shift):
+        return lax.rem(me_y + n_gy - shift, n_gy)
+
+    barrier = pltpu.get_barrier_semaphore()
+    for shift in range(1, n_gx):
+        pl.semaphore_signal(barrier, inc=1, device_id=peer_x(shift), device_id_type=MESH)
+    for shift in range(1, n_gy):
+        pl.semaphore_signal(barrier, inc=1, device_id=peer_y(shift), device_id_type=MESH)
+
+    def place(i, owner):
+        ahead = jnp.where(owner == n_gy - 1, nblk - 1, 0)
+        return lax.rem(i // levels + ahead, nblk), lax.rem(i, levels)
+
+    def load(i):
+        blk, level = place(i, me_y)
+        at = pl.ds(pl.multiple_of(blk * ROWS, ROWS), ROWS)
+        return pltpu.make_async_copy(field_ref.at[level, at], own.at[level, at], ls.at[blk, level])
+
+    def rows_x(shift, i):
+        blk, level = place(i, me_y)
+        at = pl.ds(pl.multiple_of(blk * ROWS, ROWS), ROWS)
+        return pltpu.make_async_remote_copy(
+            src_ref=field_ref.at[level, at], dst_ref=xgot.at[shift - 1, level, at],
+            send_sem=xs.at[shift - 1, blk, level], recv_sem=xr.at[shift - 1, blk, level],
+            device_id=peer_x(shift), device_id_type=MESH)
+
+    def spec_y(shift, i, source):
+        blk, level = place(i, source)
+        return pltpu.make_async_remote_copy(
+            src_ref=send.at[shift - 1, blk, level], dst_ref=got.at[source, blk, level],
+            send_sem=zs.at[shift - 1, blk, level], recv_sem=zr.at[shift - 1, blk, level],
+            device_id=peer_y(shift), device_id_type=MESH)
+
+    def edge_y(side, shift):
+        return pltpu.make_async_remote_copy(
+            src_ref=esend.at[shift], dst_ref=egot.at[side],
+            send_sem=fs.at[shift - 1], recv_sem=fr.at[side],
+            device_id=peer_y(shift), device_id_type=MESH)
+
+    @pl.loop(0, chunks)
+    def _(i):
+        load(i).start()
+
+    pl.semaphore_wait(barrier, n_gx + n_gy - 2)
+
+    @pl.loop(0, depth)
+    def _(i):
+        for shift in range(1, n_gx):
+            rows_x(shift, i).start()
+
+    norm = 1.0 / math.sqrt(length)
+    ngroup = size // GROUP
+    g = lax.broadcasted_iota(jnp.int32, (ngroup, 1), 0) * GROUP
+    shift_at = g // bands
+    first = lax.rem(me_y + shift_at, n_gy) * (n_gx * bands) + me_x * bands + (g - shift_at * bands)
+    is_cos = first < nx // 2
+    number = jnp.where(is_cos, first, first - (nx // 2 - 1)).astype(jnp.float32)
+    step = lax.broadcasted_iota(jnp.int32, (GROUP, 1), 0).astype(jnp.float32)
+
+    def factors(column):
+        c, s = unit_circle(number * column, length)
+        p, q = jnp.where(is_cos, c, -s), jnp.where(is_cos, s, c)
+        c, s = unit_circle(step * column, length)
+        return p, q, c * norm, s * norm
+
+    def expand(write, width):
+        @pl.loop(0, ngroup // 8)
+        def _(k):
+            at = pl.ds(pl.multiple_of(k * 8, 8), 8)
+            for r in range(8):
+                p, q = pq[0, at, :width][r:r + 1], pq[1, at, :width][r:r + 1]
+                write(pl.multiple_of((k * 8 + r) * GROUP, GROUP), p * cs[0, :, :width] - q * cs[1, :, :width])
+
+    for at in range(n_gx):
+        base = (lax.rem(me_x + at, n_gx) * cols).astype(jnp.float32)
+        column = lax.broadcasted_iota(jnp.int32, (1, cols), 1).astype(jnp.float32) + base
+        pq[0], pq[1], cs[0], cs[1] = factors(column)
+
+        def write(k, value, at=at):
+            tab[at, pl.ds(k, GROUP), :] = value.astype(jnp.bfloat16)
+
+        expand(write, cols)
+    lane = lax.broadcasted_iota(jnp.int32, (1, LANES), 1)
+    p, q, c, s = factors(lane.astype(jnp.float32) + float(nx))
+    pq[0, :, :LANES], pq[1, :, :LANES], cs[0, :, :LANES], cs[1, :, :LANES] = p, q, c, s
+
+    def write_zone(k, value):
+        ztab[pl.ds(k, GROUP), :] = jnp.where(lane < EXT_ZONE, value, 0.0).astype(jnp.bfloat16)
+
+    expand(write_zone, LANES)
+
+    t = jnp.minimum(lane + 1, EXT_ZONE).astype(jnp.float32) / (EXT_ZONE + 1.0)
+    cube, square = t * t * t, t * t
+    weight_a = 2.0 * cube - 3.0 * square + 1.0
+    weight_b = cube - 2.0 * square + t
+    weight_c = -2.0 * cube + 3.0 * square
+    weight_d = cube - square
+    tangent = EXT_ZONE + 1.0
+    tail = cols - LANES
+
+    def zone_of(parts):
+        first = second = last = before = 0.0
+        for at, part in enumerate(parts):
+            owner = lax.rem(me_x + at, n_gx)
+            is_first = jnp.where(owner == 0, 1.0, 0.0)
+            is_last = jnp.where(owner == n_gx - 1, 1.0, 0.0)
+            head = part[:, :LANES].astype(jnp.float32)
+            rear = part[:, tail:].astype(jnp.float32)
+            first += is_first * head[:, 0:1]
+            second += is_first * head[:, 1:2]
+            before += is_last * rear[:, LANES - 2:LANES - 1]
+            last += is_last * rear[:, LANES - 1:LANES]
+        zone = (last * weight_a + (tangent * (last - before)) * weight_b
+                + first * weight_c + (tangent * (second - first)) * weight_d)
+        return zone.astype(jnp.bfloat16)
+
+    def dot(a, b):
+        return lax.dot_general(a, b, NT, preferred_element_type=jnp.float32)
+
+    def arrive(i):
+        for shift in range(n_gy):
+            source = source_y(shift)
+            blk, level = place(i, source)
+            if shift:
+                spec_y(shift, i, source).wait_recv()
+            out_ref[source * nblk + blk, pl.ds(level, bands, stride=levels), :] = (
+                got[source, blk, level].astype(jnp.float32))
+
+    def split(i):
+        blk, level = place(i, me_y)
+        at = pl.ds(pl.multiple_of(blk * ROWS, ROWS), ROWS)
+        return blk, level, at
+
+    def own_part(i):
+        blk, level, at = split(i)
+        acc[...] = dot(tab[0], own[level, at, :])
+
+    def compute(i):
+        blk, level, at = split(i)
+        parts = [own[level, at, :]] + [xgot[x, level, at, :] for x in range(n_gx - 1)]
+        total = acc[...] + dot(ztab[...], zone_of(parts))
+        for x in range(1, n_gx):
+            total += dot(tab[x], parts[x])
+        got[me_y, blk, level] = total[:bands].astype(jnp.bfloat16)
+        for shift in range(1, n_gy):
+            send[shift - 1, blk, level] = total[shift * bands:(shift + 1) * bands].astype(jnp.bfloat16)
+
+    def edges():
+        top = me_y == 0
+        row0 = pl.multiple_of(jnp.where(top, 0, rows - 16), 16)
+        parts = [own[:, pl.ds(row0, 16), :].reshape(levels * 16, cols)]
+        parts += [xgot[x, :, pl.ds(row0, 16), :].reshape(levels * 16, cols) for x in range(n_gx - 1)]
+        total = dot(zone_of(parts), ztab[...])
+        for x, part in enumerate(parts):
+            total += dot(part, tab[x])
+        esum[...] = total
+        for pair in range(2):
+            for level in range(levels):
+                upper = esum[level * 16 + pair:level * 16 + pair + 1, :]
+                lower = esum[level * 16 + 14 + pair:level * 16 + 15 + pair, :]
+                line = jnp.where(top, upper, lower)
+                for shift in range(n_gy):
+                    esend[shift, pair, level:level + 1, :] = line[:, shift * bands:(shift + 1) * bands]
+        for side, owner in ((0, 0), (1, n_gy - 1)):
+            @pl.when(me_y == owner)
+            def _(side=side):
+                egot[side] = esend[0]
+                for shift in range(1, n_gy):
+                    edge_y(side, shift).start()
+
+    seam = (me_y == 0) | (me_y == n_gy - 1)
+
+    @pl.loop(0, chunks)
+    def _(i):
+        load(i).wait()
+        own_part(i)
+        for shift in range(1, n_gx):
+            rows_x(shift, i).wait_recv()
+
+        @pl.when(i + depth < chunks)
+        def _():
+            for shift in range(1, n_gx):
+                rows_x(shift, i + depth).start()
+
+        compute(i)
+        for shift in order:
+            spec_y(shift, i, me_y).start()
+
+        @pl.when(seam & (i == levels - 1))
+        def _():
+            edges()
+
+        @pl.when(i >= lag)
+        def _():
+            arrive(i - lag)
+
+    for side, owner in ((0, 0), (1, n_gy - 1)):
+        @pl.when(me_y != owner)
+        def _(side=side):
+            edge_y(side, 1).wait_recv()
+
+        @pl.when(me_y == owner)
+        def _(side=side):
+            for shift in range(1, n_gy):
+                edge_y(side, shift).wait_send()
+
+    wa, wb, wc, wd = host_weights(EXT_ZONE)
+    slope_start = tangent * (egot[1, 1] - egot[1, 0])
+    slope_end = tangent * (egot[0, 1] - egot[0, 0])
+    for j in range(EXT_ZONE):
+        zone_ref[j] = (egot[1, 1] * float(wa[j]) + slope_start * float(wb[j])
+                       + egot[0, 0] * float(wc[j]) + slope_end * float(wd[j]))
+
+    @pl.loop(chunks - lag, chunks)
+    def _(i):
+        arrive(i)
+
+    @pl.loop(0, chunks)
+    def _(i):
+        for shift in range(1, n_gx):
+            rows_x(shift, i).wait_send()
+        for shift in range(1, n_gy):
+            spec_y(shift, i, me_y).wait_send()
+
+
+def make_fused_body(mesh):
+    n_gx, n_gy = mesh.shape["gx"], mesh.shape["gy"]
+
+    def body(field):
+        levels, rows, cols = field.shape
+        bands = cols // n_gy
+        nblk, ny, size = rows // ROWS, rows * n_gy, n_gy * bands
+        xs, ys = n_gx - 1, n_gy - 1
+        vmem, dma = pl.BlockSpec(memory_space=pltpu.VMEM), pltpu.SemaphoreType.DMA
+        bf16, f32 = jnp.bfloat16, jnp.float32
+        spectra, zone = pl.pallas_call(
+            functools.partial(fused_kernel, n_gx, n_gy, depth=DEPTH, lag=LAG),
+            out_shape=(
+                jax.ShapeDtypeStruct((n_gy * nblk, bands * levels, ROWS), f32),
+                jax.ShapeDtypeStruct((EXT_ZONE, levels, bands), f32),
+            ),
+            in_specs=[pl.BlockSpec(memory_space=pltpu.HBM)],
+            out_specs=(vmem, vmem),
+            scratch_shapes=[
+                pltpu.VMEM((levels, rows, cols), bf16),
+                pltpu.VMEM((xs, levels, rows, cols), bf16),
+                pltpu.VMEM((n_gy, nblk, levels, bands, ROWS), bf16),
+                pltpu.VMEM((ys, nblk, levels, bands, ROWS), bf16),
+                pltpu.VMEM((n_gx, size, cols), bf16),
+                pltpu.VMEM((size, LANES), bf16),
+                pltpu.VMEM((2, size // GROUP, cols), f32),
+                pltpu.VMEM((2, GROUP, cols), f32),
+                pltpu.VMEM((size, ROWS), f32),
+                pltpu.VMEM((levels * 16, size), f32),
+                pltpu.VMEM((n_gy, 2, levels, bands), f32),
+                pltpu.VMEM((2, 2, levels, bands), f32),
+                dma((nblk, levels)),
+                dma((xs, nblk, levels)), dma((xs, nblk, levels)),
+                dma((ys, nblk, levels)), dma((ys, nblk, levels)),
+                dma((ys,)), dma((2,)),
+            ],
+            compiler_params=pltpu.CompilerParams(
+                collective_id=0, has_side_effects=True, vmem_limit_bytes=VMEM_LIMIT),
+        )(pltpu.with_memory_space_constraint(field, pltpu.HBM))
+        spectra = pl.pallas_call(
+            store_kernel,
+            out_shape=jax.ShapeDtypeStruct((bands * levels, ny), f32),
+            in_specs=[vmem],
+            out_specs=pl.BlockSpec(memory_space=pl.ANY),
+            scratch_shapes=[dma((n_gy * nblk,))],
+            compiler_params=pltpu.CompilerParams(vmem_limit_bytes=VMEM_LIMIT_STORE),
+        )(spectra)
+        return spectra.reshape(bands, levels, ny), zone.transpose(2, 1, 0)
+
+    return body
+
+
+def store_kernel(tile_ref, out_ref, sem):
+    copies = [
+        pltpu.make_async_copy(tile_ref.at[b], out_ref.at[:, pl.ds(b * ROWS, ROWS)], sem.at[b])
+        for b in range(tile_ref.shape[0])
+    ]
+    for copy in copies:
+        copy.start()
+    for copy in copies:
+        copy.wait()
+
+
+VMEM_LIMIT_STORE = 16 * 2**20
+DEPTH, LAG = 4, 3
+VMEM_LIMIT = 36 * 2**20
+
+
+def fits(mesh, shape):
+    n_gx, n_gy = mesh.shape["gx"], mesh.shape["gy"]
+    levels = shape[0] // (mesh.shape["member"] * mesh.shape["lev"])
+    rows, cols = shape[1] // n_gy, shape[2] // n_gx
+    bands = cols // n_gy
+    return (n_gx > 1 and n_gy > 1 and rows % ROWS == 0 and cols % LANES == 0 and bands % GROUP == 0 and n_gy * bands % (8 * GROUP) == 0
+            and (cols * n_gx // 2) % bands == 0 and levels % 8 == 0 and levels * rows // ROWS > DEPTH)
+
+
 def solution(mesh):
-    return jax.shard_map(
-        make_body(mesh),
-        mesh=mesh,
-        in_specs=(P(("member", "lev"), "gy", "gx"),),
-        out_specs=(
-            P(("gy", "gx"), ("member", "lev"), None),
-            P(("gy", "gx"), ("member", "lev"), None),
-        ),
-        check_vma=False,
-    )
+    def program(field):
+        body = make_fused_body(mesh) if fits(mesh, field.shape) else make_plain_body(mesh)
+        return jax.shard_map(
+            body,
+            mesh=mesh,
+            in_specs=(P(("member", "lev"), "gy", "gx"),),
+            out_specs=(
+                P(("gy", "gx"), ("member", "lev"), None),
+                P(("gy", "gx"), ("member", "lev"), None),
+            ),
+            check_vma=False,
+        )(field)
+
+    return program

time: 162 us -> 123 us (0.76)
  local copies, waits for them, and re-layouts: 21.2 us -> 0.64 us
  other arithmetic: 12.3 us -> 0 us
  Pallas kernels: 127 us -> 121 us
    dynamic_update_slice x4 -> x0, local copies, waits for them, and re-layouts: 13.2 us -> none  [body(): spectra = lax.dynamic_update_slice(spectra, full, (0, 0, source * rows))]
    convert_element_type x4 -> x0, other arithmetic: 6.51 us -> none  [the longest x1 5.52 us: body(): full = got[shift].transpose(1, 0, 2).astype(jnp.float32)]
    pallas_call x1 -> x2, Pallas kernels: 127 us -> 121 us  [the longest x1 117 us: body(): pl.pallas_call(functools.partial(fused_kernel, n_gx, n_gy, depth=DEPTH, l...]
    unnamed x4 -> x1, local copies, waits for them, and re-layouts: 4.22 us -> 0.64 us
    another operation x2 -> x0, other arithmetic: 2.21 us -> none  [the longest x1 1.61 us: body(): table = jnp.stack([expand(i * cols, (i + 1) * cols) for i in range(n_gx)])]
    select_n x4 -> x0, other arithmetic: 2.11 us -> none  [the longest x1 1.4 us: wave_factors(): p, q = (jnp.where(is_cosine, cos0, -sin0), jnp.where(is_cosine, sin0, cos0))]
where the time goes in v1:
time: 123 us; the launch traced here: 122 us
  Pallas kernels  121 us (98%)
    pallas_call x1, Pallas kernels, body(): pl.pallas_call(functools.partial(fused_kernel, n_gx, n_gy, depth=DEPTH, l...  117 us
    pallas_call x1, Pallas kernels, body(): pl.pallas_call(store_kernel, out_shape=jax.ShapeDtypeStruct((bands * leve...  3.72 us

profile of v1, /device:TPU:0, one launch (start us, length us, event | category | flops | bytes accessed | tf_op | source)
XLA Modules:
  0.0 122.4 jit_solution(820966554586034804)
XLA Ops:
  0.6 117.4 %shard_map.30 = (f32[12,1536,128]{2,1,0:T(8,128)S(1)}, f32[11,8,192]{2,1,0:T(8,128)S(1)}) custom-call(bf16[8,384,768]{2,1,0:T(8,128)(2,1)} %field_ref.1), custom_call_target="tpu_custom_call" | custom-call | tf_op jit(solution)/shard_map/pallas_call | solution.py:531
  118.1 3.7 %shard_map.31 = f32[1536,1536]{1,0:T(8,128)} custom-call(f32[12,1536,128]{2,1,0:T(8,128)S(1)} %get-tuple-element.4.tile_ref), custom_call_target="tpu_custom_call" | custom-call | tf_op jit(solution)/shard_map/pallas_call | solution.py:560
  121.8 0.6 copy.4

commit v2 on v1

--- a/solution.py
+++ b/solution.py
@@ -276,7 +276,7 @@
 
 def fused_kernel(n_gx, n_gy, field_ref, out_ref, zone_ref,
                  own, xgot, got, send, tab, ztab, pq, cs, acc, esum, esend, egot,
-                 ls, xs, xr, zs, zr, fs, fr, *, depth, lag):
+                 ls, xs, xr, zs, zr, fs, fr, far, *, depth, lag):
     levels, rows, cols = field_ref.shape
     bands = got.shape[3]
     nblk = rows // ROWS
@@ -285,7 +285,6 @@
     length = nx + EXT_ZONE
     me_x, me_y = lax.axis_index("gx"), lax.axis_index("gy")
     chunks = levels * nblk
-    order = sorted(range(1, n_gy), key=lambda shift: abs(2 * shift - n_gy))
 
     def peer_x(shift):
         return {"gx": lax.rem(me_x + n_gx - shift, n_gx)}
@@ -293,61 +292,109 @@
     def peer_y(shift):
         return {"gy": lax.rem(me_y + shift, n_gy)}
 
-    def source_y(shift):
-        return lax.rem(me_y + n_gy - shift, n_gy)
+    def turn(k):
+        up, down = n_gy - 1 - k, k
+        up = jnp.where(up > me_y, up, up - 1)
+        down = jnp.where(down < me_y, down, down + 1)
+        return lax.rem(jnp.where(2 * me_y < n_gy, up, down) - me_y + n_gy, n_gy)
+
+    above, below = me_y < n_gy - 1, me_y > 0
+
+    def tell(semaphore, up):
+        pl.semaphore_signal(semaphore, inc=1, device_id={"gy": me_y + (1 if up else -1)},
+                            device_id_type=MESH)
 
     barrier = pltpu.get_barrier_semaphore()
     for shift in range(1, n_gx):
         pl.semaphore_signal(barrier, inc=1, device_id=peer_x(shift), device_id_type=MESH)
-    for shift in range(1, n_gy):
-        pl.semaphore_signal(barrier, inc=1, device_id=peer_y(shift), device_id_type=MESH)
+    pl.when(above)(lambda: tell(barrier, True))
+    pl.when(below)(lambda: tell(barrier, False))
+
+    def vouch():
+        pl.when(above & below)(lambda: tell(far.at[0], False))
+        pl.when(above & below)(lambda: tell(far.at[1], True))
+
+    def hear():
+        for hop in range(n_gy - 2):
+            @pl.when(me_y + hop < n_gy - 2)
+            def _():
+                pl.semaphore_wait(far.at[0], 1)
+                pl.when(below)(lambda: tell(far.at[0], False))
+
+            @pl.when(me_y - hop > 1)
+            def _():
+                pl.semaphore_wait(far.at[1], 1)
+                pl.when(above)(lambda: tell(far.at[1], True))
 
     def place(i, owner):
         ahead = jnp.where(owner == n_gy - 1, nblk - 1, 0)
         return lax.rem(i // levels + ahead, nblk), lax.rem(i, levels)
 
-    def load(i):
-        blk, level = place(i, me_y)
-        at = pl.ds(pl.multiple_of(blk * ROWS, ROWS), ROWS)
-        return pltpu.make_async_copy(field_ref.at[level, at], own.at[level, at], ls.at[blk, level])
+    def lines(blk):
+        return pl.ds(pl.multiple_of(blk * ROWS, ROWS), ROWS)
+
+    def load(turn_at):
+        blk, _ = place(turn_at * levels, me_y)
+        at = lines(blk)
+        return pltpu.make_async_copy(field_ref.at[:, at], own.at[:, at], ls.at[turn_at])
 
     def rows_x(shift, i):
         blk, level = place(i, me_y)
-        at = pl.ds(pl.multiple_of(blk * ROWS, ROWS), ROWS)
+        at = lines(blk)
         return pltpu.make_async_remote_copy(
             src_ref=field_ref.at[level, at], dst_ref=xgot.at[shift - 1, level, at],
-            send_sem=xs.at[shift - 1, blk, level], recv_sem=xr.at[shift - 1, blk, level],
+            send_sem=xs.at[shift - 1], recv_sem=xr.at[i],
             device_id=peer_x(shift), device_id_type=MESH)
 
-    def spec_y(shift, i, source):
-        blk, level = place(i, source)
-        return pltpu.make_async_remote_copy(
-            src_ref=send.at[shift - 1, blk, level], dst_ref=got.at[source, blk, level],
-            send_sem=zs.at[shift - 1, blk, level], recv_sem=zr.at[shift - 1, blk, level],
-            device_id=peer_y(shift), device_id_type=MESH)
-
-    def edge_y(side, shift):
-        return pltpu.make_async_remote_copy(
-            src_ref=esend.at[shift], dst_ref=egot.at[side],
-            send_sem=fs.at[shift - 1], recv_sem=fr.at[side],
-            device_id=peer_y(shift), device_id_type=MESH)
-
-    @pl.loop(0, chunks)
-    def _(i):
-        load(i).start()
-
-    pl.semaphore_wait(barrier, n_gx + n_gy - 2)
+    def rows_in(i):
+        blk, level = place(i, me_y)
+        ref = xgot.at[:, level, lines(blk)]
+        return pltpu.make_async_remote_copy(
+            src_ref=ref, dst_ref=ref, send_sem=xs.at[0], recv_sem=xr.at[i],
+            device_id=peer_x(1), device_id_type=MESH)
+
+    def spec_y(k, i):
+        shift = turn(k)
+        blk, level = place(i, me_y)
+        return pltpu.make_async_remote_copy(
+            src_ref=send.at[k, blk, level], dst_ref=got.at[me_y, blk, level],
+            send_sem=zs, recv_sem=zr.at[i], device_id=peer_y(shift), device_id_type=MESH)
+
+    def specs_in(i):
+        return pltpu.make_async_remote_copy(
+            src_ref=send.at[:, 0, 0], dst_ref=got.at[pl.ds(0, n_gy - 1), 0, 0],
+            send_sem=zs, recv_sem=zr.at[i], device_id=peer_y(1), device_id_type=MESH)
+
+    def edge_y(side, k):
+        return pltpu.make_async_remote_copy(
+            src_ref=esend.at[k], dst_ref=egot.at[side], send_sem=fs, recv_sem=fr.at[side],
+            device_id=peer_y(turn(k)), device_id_type=MESH)
+
+    def all_sent(ref, semaphore):
+        pltpu.make_async_remote_copy(
+            src_ref=ref, dst_ref=ref, send_sem=semaphore, recv_sem=fr.at[0],
+            device_id=peer_y(1), device_id_type=MESH).wait_send()
+
+    for turn_at in range(nblk):
+        load(turn_at).start()
+
+    pl.semaphore_wait(barrier, n_gx - 1 + above.astype(jnp.int32) + below.astype(jnp.int32))
 
     @pl.loop(0, depth)
     def _(i):
         for shift in range(1, n_gx):
             rows_x(shift, i).start()
 
+    vouch()
+
     norm = 1.0 / math.sqrt(length)
     ngroup = size // GROUP
     g = lax.broadcasted_iota(jnp.int32, (ngroup, 1), 0) * GROUP
-    shift_at = g // bands
-    first = lax.rem(me_y + shift_at, n_gy) * (n_gx * bands) + me_x * bands + (g - shift_at * bands)
+    block = g // bands
+    owner = jnp.full((ngroup, 1), me_y, jnp.int32)
+    for k in range(n_gy - 1):
+        owner = jnp.where(block == k, lax.rem(me_y + turn(k), n_gy), owner)
+    first = owner * (n_gx * bands) + me_x * bands + (g - block * bands)
     is_cos = first < nx // 2
     number = jnp.where(is_cos, first, first - (nx // 2 - 1)).astype(jnp.float32)
     step = lax.broadcasted_iota(jnp.int32, (GROUP, 1), 0).astype(jnp.float32)
@@ -383,6 +430,8 @@
         ztab[pl.ds(k, GROUP), :] = jnp.where(lane < EXT_ZONE, value, 0.0).astype(jnp.bfloat16)
 
     expand(write_zone, LANES)
+
+    hear()
 
     t = jnp.minimum(lane + 1, EXT_ZONE).astype(jnp.float32) / (EXT_ZONE + 1.0)
     cube, square = t * t * t, t * t
@@ -413,11 +462,9 @@
         return lax.dot_general(a, b, NT, preferred_element_type=jnp.float32)
 
     def arrive(i):
-        for shift in range(n_gy):
-            source = source_y(shift)
+        specs_in(i).wait_recv()
+        for source in range(n_gy):
             blk, level = place(i, source)
-            if shift:
-                spec_y(shift, i, source).wait_recv()
             out_ref[source * nblk + blk, pl.ds(level, bands, stride=levels), :] = (
                 got[source, blk, level].astype(jnp.float32))
 
@@ -433,12 +480,19 @@
     def compute(i):
         blk, level, at = split(i)
         parts = [own[level, at, :]] + [xgot[x, level, at, :] for x in range(n_gx - 1)]
-        total = acc[...] + dot(ztab[...], zone_of(parts))
-        for x in range(1, n_gx):
-            total += dot(tab[x], parts[x])
-        got[me_y, blk, level] = total[:bands].astype(jnp.bfloat16)
-        for shift in range(1, n_gy):
-            send[shift - 1, blk, level] = total[shift * bands:(shift + 1) * bands].astype(jnp.bfloat16)
+        zone = zone_of(parts)
+        for lo, hi in ((0, n_gy // 2), (n_gy // 2, n_gy)):
+            at = pl.ds(lo * bands, (hi - lo) * bands)
+            total = acc[at, :] + dot(ztab[at, :], zone)
+            for x in range(1, n_gx):
+                total += dot(tab[x, at, :], parts[x])
+            for k in range(lo, hi):
+                piece = total[(k - lo) * bands:(k - lo + 1) * bands].astype(jnp.bfloat16)
+                if k == n_gy - 1:
+                    got[me_y, blk, level] = piece
+                else:
+                    send[k, blk, level] = piece
+                    spec_y(k, i).start()
 
     def edges():
         top = me_y == 0
@@ -454,23 +508,26 @@
                 upper = esum[level * 16 + pair:level * 16 + pair + 1, :]
                 lower = esum[level * 16 + 14 + pair:level * 16 + 15 + pair, :]
                 line = jnp.where(top, upper, lower)
-                for shift in range(n_gy):
-                    esend[shift, pair, level:level + 1, :] = line[:, shift * bands:(shift + 1) * bands]
+                for k in range(n_gy):
+                    esend[k, pair, level:level + 1, :] = line[:, k * bands:(k + 1) * bands]
         for side, owner in ((0, 0), (1, n_gy - 1)):
             @pl.when(me_y == owner)
             def _(side=side):
-                egot[side] = esend[0]
-                for shift in range(1, n_gy):
-                    edge_y(side, shift).start()
+                egot[side] = esend[n_gy - 1]
+                for k in range(n_gy - 1):
+                    edge_y(side, k).start()
 
     seam = (me_y == 0) | (me_y == n_gy - 1)
 
     @pl.loop(0, chunks)
     def _(i):
-        load(i).wait()
+        for turn_at in range(nblk):
+            @pl.when(i == turn_at * levels)
+            def _():
+                load(turn_at).wait()
+
         own_part(i)
-        for shift in range(1, n_gx):
-            rows_x(shift, i).wait_recv()
+        rows_in(i).wait_recv()
 
         @pl.when(i + depth < chunks)
         def _():
@@ -478,8 +535,6 @@
                 rows_x(shift, i + depth).start()
 
         compute(i)
-        for shift in order:
-            spec_y(shift, i, me_y).start()
 
         @pl.when(seam & (i == levels - 1))
         def _():
@@ -492,13 +547,9 @@
     for side, owner in ((0, 0), (1, n_gy - 1)):
         @pl.when(me_y != owner)
         def _(side=side):
-            edge_y(side, 1).wait_recv()
-
-        @pl.when(me_y == owner)
-        def _(side=side):
-            for shift in range(1, n_gy):
-                edge_y(side, shift).wait_send()
-
+            edge_y(side, 0).wait_recv()
+
+    pl.when(seam)(lambda: all_sent(esend.at[pl.ds(0, n_gy - 1)], fs))
     wa, wb, wc, wd = host_weights(EXT_ZONE)
     slope_start = tangent * (egot[1, 1] - egot[1, 0])
     slope_end = tangent * (egot[0, 1] - egot[0, 0])
@@ -506,16 +557,14 @@
         zone_ref[j] = (egot[1, 1] * float(wa[j]) + slope_start * float(wb[j])
                        + egot[0, 0] * float(wc[j]) + slope_end * float(wd[j]))
 
+    for shift in range(1, n_gx):
+        all_sent(field_ref, xs.at[shift - 1])
+
     @pl.loop(chunks - lag, chunks)
     def _(i):
         arrive(i)
 
-    @pl.loop(0, chunks)
-    def _(i):
-        for shift in range(1, n_gx):
-            rows_x(shift, i).wait_send()
-        for shift in range(1, n_gy):
-            spec_y(shift, i, me_y).wait_send()
+    all_sent(send, zs)
 
 
 def make_fused_body(mesh):
@@ -549,32 +598,35 @@
                 pltpu.VMEM((levels * 16, size), f32),
                 pltpu.VMEM((n_gy, 2, levels, bands), f32),
                 pltpu.VMEM((2, 2, levels, bands), f32),
-                dma((nblk, levels)),
-                dma((xs, nblk, levels)), dma((xs, nblk, levels)),
-                dma((ys, nblk, levels)), dma((ys, nblk, levels)),
-                dma((ys,)), dma((2,)),
+                dma((nblk,)), dma((xs,)), dma((levels * nblk,)), dma, dma((levels * nblk,)),
+                dma, dma((2,)), pltpu.SemaphoreType.REGULAR((2,)),
             ],
             compiler_params=pltpu.CompilerParams(
                 collective_id=0, has_side_effects=True, vmem_limit_bytes=VMEM_LIMIT),
         )(pltpu.with_memory_space_constraint(field, pltpu.HBM))
-        spectra = pl.pallas_call(
+        spectra, zone = pl.pallas_call(
             store_kernel,
-            out_shape=jax.ShapeDtypeStruct((bands * levels, ny), f32),
-            in_specs=[vmem],
-            out_specs=pl.BlockSpec(memory_space=pl.ANY),
-            scratch_shapes=[dma((n_gy * nblk,))],
+            out_shape=(
+                jax.ShapeDtypeStruct((bands * levels, ny), f32),
+                jax.ShapeDtypeStruct(zone.shape, f32),
+            ),
+            in_specs=[vmem, vmem],
+            out_specs=(pl.BlockSpec(memory_space=pl.ANY),) * 2,
+            scratch_shapes=[dma((n_gy * nblk + 1,))],
             compiler_params=pltpu.CompilerParams(vmem_limit_bytes=VMEM_LIMIT_STORE),
-        )(spectra)
+        )(spectra, zone)
         return spectra.reshape(bands, levels, ny), zone.transpose(2, 1, 0)
 
     return body
 
 
-def store_kernel(tile_ref, out_ref, sem):
+def store_kernel(tile_ref, zone_ref, out_ref, zone_out_ref, sem):
+    count = tile_ref.shape[0]
     copies = [
         pltpu.make_async_copy(tile_ref.at[b], out_ref.at[:, pl.ds(b * ROWS, ROWS)], sem.at[b])
-        for b in range(tile_ref.shape[0])
+        for b in range(count)
     ]
+    copies.append(pltpu.make_async_copy(zone_ref, zone_out_ref, sem.at[count]))
     for copy in copies:
         copy.start()
     for copy in copies:
@@ -582,7 +634,8 @@
 
 
 VMEM_LIMIT_STORE = 16 * 2**20
-DEPTH, LAG = 4, 3
+DEPTH = 4
+LAG = 6
 VMEM_LIMIT = 36 * 2**20
 
 

time: 123 us -> 119 us (0.967)
  Pallas kernels: 121 us -> 119 us
    pallas_call x1, Pallas kernels: 117 us -> 115 us  [body(): pl.pallas_call(functools.partial(fused_kernel, n_gx, n_gy, depth=DEPTH, l...]
where the time goes in v2:
time: 119 us
  Pallas kernels  119 us (100%)
    pallas_call x1, Pallas kernels, body(): pl.pallas_call(functools.partial(fused_kernel, n_gx, n_gy, depth=DEPTH, l...  115 us
    pallas_call x1, Pallas kernels, body(): pl.pallas_call(store_kernel, out_shape=(jax.ShapeDtypeStruct((bands * lev...  3.73 us

profile of v2, /device:TPU:0, one launch (start us, length us, event | category | flops | bytes accessed | tf_op | source)
XLA Modules:
  0.0 119.2 jit_solution(5011756262398012656)
XLA Ops:
  0.6 114.9 %shard_map.30 = (f32[12,1536,128]{2,1,0:T(8,128)S(1)}, f32[11,8,192]{2,1,0:T(8,128)S(1)}) custom-call(bf16[8,384,768]{2,1,0:T(8,128)(2,1)} %field_ref.1), custom_call_target="tpu_custom_call" | custom-call | tf_op jit(solution)/shard_map/pallas_call | solution.py:580
  115.5 3.7 %shard_map.31 = (f32[1536,1536]{1,0:T(8,128)}, f32[11,8,192]{2,1,0:T(8,128)}) custom-call(f32[12,1536,128]{2,1,0:T(8,128)S(1)} %get-tuple-element.6.tile_ref, f32[11,8,192]{2,1,0:T(8,128)S(1)} %get-tuple-element.7.zone_ref), custom_call_target="tpu_custom_call" | custom-call | tf_op jit(solution)/shard_map/pallas_call | solution.py:607

commit v3 on v2

--- a/solution.py
+++ b/solution.py
@@ -275,16 +275,18 @@
 
 
 def fused_kernel(n_gx, n_gy, field_ref, out_ref, zone_ref,
-                 own, xgot, got, send, tab, ztab, pq, cs, acc, esum, esend, egot,
+                 own, xgot, got, send, tab, ztab, zbuf, pq, cs, acc, esum, esend, egot,
                  ls, xs, xr, zs, zr, fs, fr, far, *, depth, lag):
     levels, rows, cols = field_ref.shape
-    bands = got.shape[3]
-    nblk = rows // ROWS
-    size = n_gy * bands
+    bands = got.shape[2]
+    nblk, share = rows // ROWS, levels // n_gx
+    half = n_gy // 2 * n_gx * bands
     nx = n_gx * cols
     length = nx + EXT_ZONE
     me_x, me_y = lax.axis_index("gx"), lax.axis_index("gy")
-    chunks = levels * nblk
+    chunks = share * nblk
+    blocks = [(k, x) for k in range(n_gy - 1) for x in range(n_gx)]
+    blocks += [(n_gy - 1, x) for x in range(1, n_gx)] + [(n_gy - 1, 0)]
 
     def peer_x(shift):
         return {"gx": lax.rem(me_x + n_gx - shift, n_gx)}
@@ -294,6 +296,8 @@
 
     def turn(k):
         up, down = n_gy - 1 - k, k
+        if k == n_gy - 1:
+            return 0
         up = jnp.where(up > me_y, up, up - 1)
         down = jnp.where(down < me_y, down, down + 1)
         return lax.rem(jnp.where(2 * me_y < n_gy, up, down) - me_y + n_gy, n_gy)
@@ -326,25 +330,30 @@
                 pl.semaphore_wait(far.at[1], 1)
                 pl.when(above)(lambda: tell(far.at[1], True))
 
+        for shift in range(1, n_gx):
+            pl.semaphore_signal(far.at[2], inc=1, device_id=peer_x(shift), device_id_type=MESH)
+        pl.semaphore_wait(far.at[2], n_gx - 1)
+
     def place(i, owner):
         ahead = jnp.where(owner == n_gy - 1, nblk - 1, 0)
-        return lax.rem(i // levels + ahead, nblk), lax.rem(i, levels)
+        return lax.rem(i // share + ahead, nblk), lax.rem(i, share)
 
     def lines(blk):
         return pl.ds(pl.multiple_of(blk * ROWS, ROWS), ROWS)
 
     def load(turn_at):
-        blk, _ = place(turn_at * levels, me_y)
+        blk, _ = place(turn_at * share, me_y)
         at = lines(blk)
-        return pltpu.make_async_copy(field_ref.at[:, at], own.at[:, at], ls.at[turn_at])
+        return pltpu.make_async_copy(
+            field_ref.at[pl.ds(me_x * share, share), at], own.at[:, at], ls.at[turn_at])
 
     def rows_x(shift, i):
         blk, level = place(i, me_y)
         at = lines(blk)
-        return pltpu.make_async_remote_copy(
-            src_ref=field_ref.at[level, at], dst_ref=xgot.at[shift - 1, level, at],
-            send_sem=xs.at[shift - 1], recv_sem=xr.at[i],
-            device_id=peer_x(shift), device_id_type=MESH)
+        peer = peer_x(shift)
+        return pltpu.make_async_remote_copy(
+            src_ref=field_ref.at[peer["gx"] * share + level, at], dst_ref=xgot.at[shift - 1, level, at],
+            send_sem=xs.at[shift - 1], recv_sem=xr.at[i], device_id=peer, device_id_type=MESH)
 
     def rows_in(i):
         blk, level = place(i, me_y)
@@ -353,26 +362,33 @@
             src_ref=ref, dst_ref=ref, send_sem=xs.at[0], recv_sem=xr.at[i],
             device_id=peer_x(1), device_id_type=MESH)
 
-    def spec_y(k, i):
-        shift = turn(k)
-        blk, level = place(i, me_y)
-        return pltpu.make_async_remote_copy(
-            src_ref=send.at[k, blk, level], dst_ref=got.at[me_y, blk, level],
-            send_sem=zs, recv_sem=zr.at[i], device_id=peer_y(shift), device_id_type=MESH)
+    def owner_of(b):
+        k, x = blocks[b]
+        return {"gy": lax.rem(me_y + turn(k), n_gy), "gx": lax.rem(me_x + x, n_gx)}
+
+    def spec(b, i):
+        return pltpu.make_async_remote_copy(
+            src_ref=send.at[b, i], dst_ref=got.at[me_y * n_gx + me_x, i],
+            send_sem=zs, recv_sem=zr.at[i], device_id=owner_of(b), device_id_type=MESH)
 
     def specs_in(i):
         return pltpu.make_async_remote_copy(
-            src_ref=send.at[:, 0, 0], dst_ref=got.at[pl.ds(0, n_gy - 1), 0, 0],
+            src_ref=send.at[:, 0], dst_ref=got.at[pl.ds(0, len(blocks) - 1), 0],
             send_sem=zs, recv_sem=zr.at[i], device_id=peer_y(1), device_id_type=MESH)
 
-    def edge_y(side, k):
-        return pltpu.make_async_remote_copy(
-            src_ref=esend.at[k], dst_ref=egot.at[side], send_sem=fs, recv_sem=fr.at[side],
-            device_id=peer_y(turn(k)), device_id_type=MESH)
+    def edge(side, b):
+        return pltpu.make_async_remote_copy(
+            src_ref=esend.at[b], dst_ref=egot.at[side, me_x], send_sem=fs, recv_sem=fr.at[side, me_x],
+            device_id=owner_of(b), device_id_type=MESH)
+
+    def edge_in(side, x):
+        return pltpu.make_async_remote_copy(
+            src_ref=esend.at[0], dst_ref=egot.at[side, x], send_sem=fs, recv_sem=fr.at[side, x],
+            device_id=peer_y(1), device_id_type=MESH)
 
     def all_sent(ref, semaphore):
         pltpu.make_async_remote_copy(
-            src_ref=ref, dst_ref=ref, send_sem=semaphore, recv_sem=fr.at[0],
+            src_ref=ref, dst_ref=ref, send_sem=semaphore, recv_sem=fr.at[0, 0],
             device_id=peer_y(1), device_id_type=MESH).wait_send()
 
     for turn_at in range(nblk):
@@ -380,58 +396,64 @@
 
     pl.semaphore_wait(barrier, n_gx - 1 + above.astype(jnp.int32) + below.astype(jnp.int32))
 
-    @pl.loop(0, depth)
-    def _(i):
-        for shift in range(1, n_gx):
-            rows_x(shift, i).start()
-
+    def send_ahead():
+        @pl.loop(0, depth)
+        def _(i):
+            for shift in range(1, n_gx):
+                rows_x(shift, i).start()
+
+    leads = lax.axis_index("lev") != 0
+    pl.when(leads)(send_ahead)
     vouch()
 
     norm = 1.0 / math.sqrt(length)
-    ngroup = size // GROUP
-    g = lax.broadcasted_iota(jnp.int32, (ngroup, 1), 0) * GROUP
-    block = g // bands
-    owner = jnp.full((ngroup, 1), me_y, jnp.int32)
-    for k in range(n_gy - 1):
-        owner = jnp.where(block == k, lax.rem(me_y + turn(k), n_gy), owner)
-    first = owner * (n_gx * bands) + me_x * bands + (g - block * bands)
-    is_cos = first < nx // 2
-    number = jnp.where(is_cos, first, first - (nx // 2 - 1)).astype(jnp.float32)
-    step = lax.broadcasted_iota(jnp.int32, (GROUP, 1), 0).astype(jnp.float32)
-
-    def factors(column):
-        c, s = unit_circle(number * column, length)
-        p, q = jnp.where(is_cos, c, -s), jnp.where(is_cos, s, c)
-        c, s = unit_circle(step * column, length)
-        return p, q, c * norm, s * norm
-
-    def expand(write, width):
-        @pl.loop(0, ngroup // 8)
-        def _(k):
-            at = pl.ds(pl.multiple_of(k * 8, 8), 8)
-            for r in range(8):
-                p, q = pq[0, at, :width][r:r + 1], pq[1, at, :width][r:r + 1]
-                write(pl.multiple_of((k * 8 + r) * GROUP, GROUP), p * cs[0, :, :width] - q * cs[1, :, :width])
-
-    for at in range(n_gx):
-        base = (lax.rem(me_x + at, n_gx) * cols).astype(jnp.float32)
-        column = lax.broadcasted_iota(jnp.int32, (1, cols), 1).astype(jnp.float32) + base
-        pq[0], pq[1], cs[0], cs[1] = factors(column)
-
-        def write(k, value, at=at):
-            tab[at, pl.ds(k, GROUP), :] = value.astype(jnp.bfloat16)
-
-        expand(write, cols)
+    ngroup = half // GROUP
     lane = lax.broadcasted_iota(jnp.int32, (1, LANES), 1)
-    p, q, c, s = factors(lane.astype(jnp.float32) + float(nx))
-    pq[0, :, :LANES], pq[1, :, :LANES], cs[0, :, :LANES], cs[1, :, :LANES] = p, q, c, s
-
-    def write_zone(k, value):
-        ztab[pl.ds(k, GROUP), :] = jnp.where(lane < EXT_ZONE, value, 0.0).astype(jnp.bfloat16)
-
-    expand(write_zone, LANES)
-
-    hear()
+
+    def build(part):
+        row0 = part * half
+        g = lax.broadcasted_iota(jnp.int32, (ngroup, 1), 0) * GROUP + row0
+        block = g // bands
+        origin = jnp.zeros((ngroup, 1), jnp.int32)
+        for b in range(row0 // bands, (row0 + half) // bands):
+            to = owner_of(b)
+            origin = jnp.where(block == b, (to["gy"] * n_gx + to["gx"]) * bands, origin)
+        first = origin + (g - block * bands)
+        is_cos = first < nx // 2
+        number = jnp.where(is_cos, first, first - (nx // 2 - 1)).astype(jnp.float32)
+        step = lax.broadcasted_iota(jnp.int32, (GROUP, 1), 0).astype(jnp.float32)
+
+        def factors(column, width):
+            c, s = unit_circle(number * column, length)
+            pq[0, :, :width], pq[1, :, :width] = jnp.where(is_cos, c, -s), jnp.where(is_cos, s, c)
+            c, s = unit_circle(step * column, length)
+            cs[0, :, :width], cs[1, :, :width] = c * norm, s * norm
+
+        def expand(write, width):
+            @pl.loop(0, ngroup // 8)
+            def _(k):
+                at = pl.ds(pl.multiple_of(k * 8, 8), 8)
+                for r in range(8):
+                    p, q = pq[0, at, :width][r:r + 1], pq[1, at, :width][r:r + 1]
+                    write(pl.ds(pl.multiple_of(row0 + (k * 8 + r) * GROUP, GROUP), GROUP),
+                          p * cs[0, :, :width] - q * cs[1, :, :width])
+
+        for at in range(n_gx):
+            base = (lax.rem(me_x + at, n_gx) * cols).astype(jnp.float32)
+            factors(lax.broadcasted_iota(jnp.int32, (1, cols), 1).astype(jnp.float32) + base, cols)
+
+            def write(to, value, at=at):
+                tab[at, to, :] = value.astype(jnp.bfloat16)
+
+            expand(write, cols)
+            if part == 0 and at == 0:
+                pl.when(jnp.logical_not(leads))(send_ahead)
+        factors(lane.astype(jnp.float32) + float(nx), LANES)
+
+        def write_zone(to, value):
+            ztab[to, :] = jnp.where(lane < EXT_ZONE, value, 0.0).astype(jnp.bfloat16)
+
+        expand(write_zone, LANES)
 
     t = jnp.minimum(lane + 1, EXT_ZONE).astype(jnp.float32) / (EXT_ZONE + 1.0)
     cube, square = t * t * t, t * t
@@ -463,70 +485,70 @@
 
     def arrive(i):
         specs_in(i).wait_recv()
-        for source in range(n_gy):
-            blk, level = place(i, source)
-            out_ref[source * nblk + blk, pl.ds(level, bands, stride=levels), :] = (
-                got[source, blk, level].astype(jnp.float32))
-
-    def split(i):
+        for source in range(n_gy * n_gx):
+            blk, level = place(i, source // n_gx)
+            level += source % n_gx * share
+            out_ref[source // n_gx * nblk + blk, pl.ds(level, bands, stride=levels), :] = (
+                got[source, i].astype(jnp.float32))
+
+    def own_part(i, part):
         blk, level = place(i, me_y)
-        at = pl.ds(pl.multiple_of(blk * ROWS, ROWS), ROWS)
-        return blk, level, at
-
-    def own_part(i):
-        blk, level, at = split(i)
-        acc[...] = dot(tab[0], own[level, at, :])
-
-    def compute(i):
-        blk, level, at = split(i)
-        parts = [own[level, at, :]] + [xgot[x, level, at, :] for x in range(n_gx - 1)]
-        zone = zone_of(parts)
-        for lo, hi in ((0, n_gy // 2), (n_gy // 2, n_gy)):
-            at = pl.ds(lo * bands, (hi - lo) * bands)
-            total = acc[at, :] + dot(ztab[at, :], zone)
-            for x in range(1, n_gx):
-                total += dot(tab[x, at, :], parts[x])
-            for k in range(lo, hi):
-                piece = total[(k - lo) * bands:(k - lo + 1) * bands].astype(jnp.bfloat16)
-                if k == n_gy - 1:
-                    got[me_y, blk, level] = piece
-                else:
-                    send[k, blk, level] = piece
-                    spec_y(k, i).start()
+        at = pl.ds(part * half, half)
+        acc[at, :] = dot(tab[0, at, :], own[level, lines(blk), :])
+
+    def blend(i):
+        blk, level = place(i, me_y)
+        at = lines(blk)
+        zbuf[...] = zone_of([own[level, at, :]] + [xgot[x, level, at, :] for x in range(n_gx - 1)])
+
+    def finish(i, lo, hi):
+        blk, level = place(i, me_y)
+        at = pl.ds(lo * bands, (hi - lo) * bands)
+        total = acc[at, :] + dot(ztab[at, :], zbuf[...])
+        for x in range(1, n_gx):
+            total += dot(tab[x, at, :], xgot[x - 1, level, lines(blk), :])
+        for b in range(lo, hi):
+            piece = total[(b - lo) * bands:(b - lo + 1) * bands].astype(jnp.bfloat16)
+            if b == len(blocks) - 1:
+                got[me_y * n_gx + me_x, i] = piece
+            else:
+                send[b, i] = piece
+                spec(b, i).start()
+
+    def far_pieces(i):
+        for lo in range(0, half // bands, n_gx):
+            finish(i, lo, lo + n_gx)
+
+    def near_pieces(i):
+        finish(i, half // bands, len(blocks))
 
     def edges():
         top = me_y == 0
         row0 = pl.multiple_of(jnp.where(top, 0, rows - 16), 16)
-        parts = [own[:, pl.ds(row0, 16), :].reshape(levels * 16, cols)]
-        parts += [xgot[x, :, pl.ds(row0, 16), :].reshape(levels * 16, cols) for x in range(n_gx - 1)]
+        parts = [own[:, pl.ds(row0, 16), :].reshape(share * 16, cols)]
+        parts += [xgot[x, :, pl.ds(row0, 16), :].reshape(share * 16, cols) for x in range(n_gx - 1)]
         total = dot(zone_of(parts), ztab[...])
         for x, part in enumerate(parts):
             total += dot(part, tab[x])
         esum[...] = total
         for pair in range(2):
-            for level in range(levels):
+            for level in range(share):
                 upper = esum[level * 16 + pair:level * 16 + pair + 1, :]
                 lower = esum[level * 16 + 14 + pair:level * 16 + 15 + pair, :]
                 line = jnp.where(top, upper, lower)
-                for k in range(n_gy):
-                    esend[k, pair, level:level + 1, :] = line[:, k * bands:(k + 1) * bands]
+                row = pair * share + level
+                for b in range(len(blocks)):
+                    esend[b, row:row + 1, :] = line[:, b * bands:(b + 1) * bands]
         for side, owner in ((0, 0), (1, n_gy - 1)):
             @pl.when(me_y == owner)
             def _(side=side):
-                egot[side] = esend[n_gy - 1]
-                for k in range(n_gy - 1):
-                    edge_y(side, k).start()
+                egot[side, me_x] = esend[len(blocks) - 1]
+                for b in range(len(blocks) - 1):
+                    edge(side, b).start()
 
     seam = (me_y == 0) | (me_y == n_gy - 1)
 
-    @pl.loop(0, chunks)
-    def _(i):
-        for turn_at in range(nblk):
-            @pl.when(i == turn_at * levels)
-            def _():
-                load(turn_at).wait()
-
-        own_part(i)
+    def rows_ready(i):
         rows_in(i).wait_recv()
 
         @pl.when(i + depth < chunks)
@@ -534,9 +556,32 @@
             for shift in range(1, n_gx):
                 rows_x(shift, i + depth).start()
 
-        compute(i)
-
-        @pl.when(seam & (i == levels - 1))
+        blend(i)
+
+    build(0)
+    load(0).wait()
+    own_part(0, 0)
+    hear()
+    rows_ready(0)
+    far_pieces(0)
+    build(1)
+    own_part(0, 1)
+    near_pieces(0)
+
+    @pl.loop(1, chunks)
+    def _(i):
+        for turn_at in range(1, nblk):
+            @pl.when(i == turn_at * share)
+            def _():
+                load(turn_at).wait()
+
+        own_part(i, 0)
+        own_part(i, 1)
+        rows_ready(i)
+        far_pieces(i)
+        near_pieces(i)
+
+        @pl.when(seam & (i == share - 1))
         def _():
             edges()
 
@@ -545,20 +590,24 @@
             arrive(i - lag)
 
     for side, owner in ((0, 0), (1, n_gy - 1)):
-        @pl.when(me_y != owner)
-        def _(side=side):
-            edge_y(side, 0).wait_recv()
-
-    pl.when(seam)(lambda: all_sent(esend.at[pl.ds(0, n_gy - 1)], fs))
+        for x in range(n_gx):
+            @pl.when((me_y != owner) | (me_x != x))
+            def _(side=side, x=x):
+                edge_in(side, x).wait_recv()
+
+    pl.when(seam)(lambda: all_sent(esend.at[pl.ds(0, len(blocks) - 1)], fs))
     wa, wb, wc, wd = host_weights(EXT_ZONE)
-    slope_start = tangent * (egot[1, 1] - egot[1, 0])
-    slope_end = tangent * (egot[0, 1] - egot[0, 0])
-    for j in range(EXT_ZONE):
-        zone_ref[j] = (egot[1, 1] * float(wa[j]) + slope_start * float(wb[j])
-                       + egot[0, 0] * float(wc[j]) + slope_end * float(wd[j]))
+    for x in range(n_gx):
+        first, second = egot[0, x, :share, :], egot[0, x, share:, :]
+        before, last = egot[1, x, :share, :], egot[1, x, share:, :]
+        slope_start, slope_end = tangent * (last - before), tangent * (second - first)
+        for j in range(EXT_ZONE):
+            zone_ref[j, x * share:(x + 1) * share, :] = (
+                last * float(wa[j]) + slope_start * float(wb[j])
+                + first * float(wc[j]) + slope_end * float(wd[j]))
 
     for shift in range(1, n_gx):
-        all_sent(field_ref, xs.at[shift - 1])
+        all_sent(field_ref.at[pl.ds(0, share)], xs.at[shift - 1])
 
     @pl.loop(chunks - lag, chunks)
     def _(i):
@@ -573,8 +622,9 @@
     def body(field):
         levels, rows, cols = field.shape
         bands = cols // n_gy
-        nblk, ny, size = rows // ROWS, rows * n_gy, n_gy * bands
-        xs, ys = n_gx - 1, n_gy - 1
+        nblk, ny, size = rows // ROWS, rows * n_gy, n_gy * n_gx * bands
+        share, xs, peers = levels // n_gx, n_gx - 1, n_gy * n_gx - 1
+        chunks = share * nblk
         vmem, dma = pl.BlockSpec(memory_space=pltpu.VMEM), pltpu.SemaphoreType.DMA
         bf16, f32 = jnp.bfloat16, jnp.float32
         spectra, zone = pl.pallas_call(
@@ -586,20 +636,21 @@
             in_specs=[pl.BlockSpec(memory_space=pltpu.HBM)],
             out_specs=(vmem, vmem),
             scratch_shapes=[
-                pltpu.VMEM((levels, rows, cols), bf16),
-                pltpu.VMEM((xs, levels, rows, cols), bf16),
-                pltpu.VMEM((n_gy, nblk, levels, bands, ROWS), bf16),
-                pltpu.VMEM((ys, nblk, levels, bands, ROWS), bf16),
+                pltpu.VMEM((share, rows, cols), bf16),
+                pltpu.VMEM((xs, share, rows, cols), bf16),
+                pltpu.VMEM((peers + 1, chunks, bands, ROWS), bf16),
+                pltpu.VMEM((peers, chunks, bands, ROWS), bf16),
                 pltpu.VMEM((n_gx, size, cols), bf16),
                 pltpu.VMEM((size, LANES), bf16),
-                pltpu.VMEM((2, size // GROUP, cols), f32),
+                pltpu.VMEM((ROWS, LANES), bf16),
+                pltpu.VMEM((2, size // 2 // GROUP, cols), f32),
                 pltpu.VMEM((2, GROUP, cols), f32),
                 pltpu.VMEM((size, ROWS), f32),
-                pltpu.VMEM((levels * 16, size), f32),
-                pltpu.VMEM((n_gy, 2, levels, bands), f32),
-                pltpu.VMEM((2, 2, levels, bands), f32),
-                dma((nblk,)), dma((xs,)), dma((levels * nblk,)), dma, dma((levels * nblk,)),
-                dma, dma((2,)), pltpu.SemaphoreType.REGULAR((2,)),
+                pltpu.VMEM((share * 16, size), f32),
+                pltpu.VMEM((peers + 1, 2 * share, bands), f32),
+                pltpu.VMEM((2, n_gx, 2 * share, bands), f32),
+                dma((nblk,)), dma((xs,)), dma((chunks,)), dma, dma((chunks,)),
+                dma, dma((2, n_gx)), pltpu.SemaphoreType.REGULAR((3,)),
             ],
             compiler_params=pltpu.CompilerParams(
                 collective_id=0, has_side_effects=True, vmem_limit_bytes=VMEM_LIMIT),
@@ -634,8 +685,8 @@
 
 
 VMEM_LIMIT_STORE = 16 * 2**20
-DEPTH = 4
-LAG = 6
+DEPTH = 3
+LAG = 3
 VMEM_LIMIT = 36 * 2**20
 
 
@@ -644,8 +695,10 @@
     levels = shape[0] // (mesh.shape["member"] * mesh.shape["lev"])
     rows, cols = shape[1] // n_gy, shape[2] // n_gx
     bands = cols // n_gy
-    return (n_gx > 1 and n_gy > 1 and rows % ROWS == 0 and cols % LANES == 0 and bands % GROUP == 0 and n_gy * bands % (8 * GROUP) == 0
-            and (cols * n_gx // 2) % bands == 0 and levels % 8 == 0 and levels * rows // ROWS > DEPTH)
+    return (n_gx > 1 and n_gy > 1 and n_gy % 2 == 0 and rows % ROWS == 0 and cols % LANES == 0
+            and bands % GROUP == 0 and n_gy * n_gx * bands % (16 * GROUP) == 0
+            and (cols * n_gx // 2) % bands == 0 and levels % 8 == 0 and levels % (2 * n_gx) == 0
+            and levels // n_gx * rows // ROWS > max(DEPTH, LAG))
 
 
 def solution(mesh):

time: 119 us -> 118 us (level)
  Pallas kernels: 119 us -> 117 us
where the time goes in v3:
time: 118 us
  Pallas kernels  117 us (99%)
    pallas_call x1, Pallas kernels, body(): pl.pallas_call(functools.partial(fused_kernel, n_gx, n_gy, depth=DEPTH, l...  114 us
    pallas_call x1, Pallas kernels, body(): pl.pallas_call(store_kernel, out_shape=(jax.ShapeDtypeStruct((bands * lev...  3.73 us

profile of v3, /device:TPU:0, one launch (start us, length us, event | category | flops | bytes accessed | tf_op | source)
XLA Modules:
  0.0 118.1 jit_solution(18013930657973365833)
XLA Ops:
  0.6 113.7 %shard_map.30 = (f32[12,1536,128]{2,1,0:T(8,128)S(1)}, f32[11,8,192]{2,1,0:T(8,128)S(1)}) custom-call(bf16[8,384,768]{2,1,0:T(8,128)(2,1)} %field_ref.1), custom_call_target="tpu_custom_call" | custom-call | tf_op jit(solution)/shard_map/pallas_call | solution.py:630
  114.4 3.7 %shard_map.31 = (f32[1536,1536]{1,0:T(8,128)}, f32[11,8,192]{2,1,0:T(8,128)}) custom-call(f32[12,1536,128]{2,1,0:T(8,128)S(1)} %get-tuple-element.6.tile_ref, f32[11,8,192]{2,1,0:T(8,128)S(1)} %get-tuple-element.7.zone_ref), custom_call_target="tpu_custom_call" | custom-call | tf_op jit(solution)/shard_map/pallas_call | solution.py:658

commit v4 on v3

--- a/solution.py
+++ b/solution.py
@@ -276,7 +276,7 @@
 
 def fused_kernel(n_gx, n_gy, field_ref, out_ref, zone_ref,
                  own, xgot, got, send, tab, ztab, zbuf, pq, cs, acc, esum, esend, egot,
-                 ls, xs, xr, zs, zr, fs, fr, far, *, depth, lag):
+                 ls, xs, xr, zs, zr, fs, fr, far, *, depth, lags):
     levels, rows, cols = field_ref.shape
     bands = got.shape[2]
     nblk, share = rows // ROWS, levels // n_gx
@@ -403,6 +403,7 @@
                 rows_x(shift, i).start()
 
     leads = lax.axis_index("lev") != 0
+    lag = jnp.where(leads, *lags)
     pl.when(leads)(send_ahead)
     vouch()
 
@@ -628,7 +629,7 @@
         vmem, dma = pl.BlockSpec(memory_space=pltpu.VMEM), pltpu.SemaphoreType.DMA
         bf16, f32 = jnp.bfloat16, jnp.float32
         spectra, zone = pl.pallas_call(
-            functools.partial(fused_kernel, n_gx, n_gy, depth=DEPTH, lag=LAG),
+            functools.partial(fused_kernel, n_gx, n_gy, depth=DEPTH, lags=(LAG_LEAD, LAG)),
             out_shape=(
                 jax.ShapeDtypeStruct((n_gy * nblk, bands * levels, ROWS), f32),
                 jax.ShapeDtypeStruct((EXT_ZONE, levels, bands), f32),
@@ -686,6 +687,7 @@
 
 VMEM_LIMIT_STORE = 16 * 2**20
 DEPTH = 3
+LAG_LEAD = 1
 LAG = 3
 VMEM_LIMIT = 36 * 2**20
 

time: 118 us -> 117 us (level); the launches traced: 118 us -> 116 us
  Pallas kernels: 117 us -> 115 us
    pallas_call x1, Pallas kernels: 114 us -> 111 us  [body(): pl.pallas_call(functools.partial(fused_kernel, n_gx, n_gy, depth=DEPTH, l...]
where the time goes in v4:
time: 117 us; the launch traced here: 116 us
  Pallas kernels  115 us (98%)
    pallas_call x1, Pallas kernels, body(): pl.pallas_call(functools.partial(fused_kernel, n_gx, n_gy, depth=DEPTH, l...  111 us
    pallas_call x1, Pallas kernels, body(): pl.pallas_call(store_kernel, out_shape=(jax.ShapeDtypeStruct((bands * lev...  3.73 us

profile of v4, /device:TPU:0, one launch (start us, length us, event | category | flops | bytes accessed | tf_op | source)
XLA Modules:
  0.0 115.5 jit_solution(16781738494865675680)
XLA Ops:
  0.6 111.2 %shard_map.30 = (f32[12,1536,128]{2,1,0:T(8,128)S(1)}, f32[11,8,192]{2,1,0:T(8,128)S(1)}) custom-call(bf16[8,384,768]{2,1,0:T(8,128)(2,1)} %field_ref.1), custom_call_target="tpu_custom_call" | custom-call | tf_op jit(solution)/shard_map/pallas_call | solution.py:631
  111.8 3.7 %shard_map.31 = (f32[1536,1536]{1,0:T(8,128)}, f32[11,8,192]{2,1,0:T(8,128)}) custom-call(f32[12,1536,128]{2,1,0:T(8,128)S(1)} %get-tuple-element.6.tile_ref, f32[11,8,192]{2,1,0:T(8,128)S(1)} %get-tuple-element.7.zone_ref), custom_call_target="tpu_custom_call" | custom-call | tf_op jit(solution)/shard_map/pallas_call | solution.py:659

commit v5 on v4

--- a/solution.py
+++ b/solution.py
@@ -275,8 +275,8 @@
 
 
 def fused_kernel(n_gx, n_gy, field_ref, out_ref, zone_ref,
-                 own, xgot, got, send, tab, ztab, zbuf, pq, cs, acc, esum, esend, egot,
-                 ls, xs, xr, zs, zr, fs, fr, far, *, depth, lags):
+                 own, staged, xgot, got, send, tab, ztab, zbuf, pq, cs, acc, esum, esend, egot,
+                 ss, ls, xs, xr, zs, zr, fs, fr, far, *, depth, lags):
     levels, rows, cols = field_ref.shape
     bands = got.shape[2]
     nblk, share = rows // ROWS, levels // n_gx
@@ -347,12 +347,19 @@
         return pltpu.make_async_copy(
             field_ref.at[pl.ds(me_x * share, share), at], own.at[:, at], ls.at[turn_at])
 
-    def rows_x(shift, i):
+    def stage(shift):
+        blk, _ = place(0, me_y)
+        return pltpu.make_async_copy(
+            field_ref.at[peer_x(shift)["gx"] * share, lines(blk)], staged.at[shift - 1], ss.at[shift - 1])
+
+    def rows_x(shift, i, source=None):
         blk, level = place(i, me_y)
         at = lines(blk)
         peer = peer_x(shift)
-        return pltpu.make_async_remote_copy(
-            src_ref=field_ref.at[peer["gx"] * share + level, at], dst_ref=xgot.at[shift - 1, level, at],
+        if source is None:
+            source = field_ref.at[peer["gx"] * share + level, at]
+        return pltpu.make_async_remote_copy(
+            src_ref=source, dst_ref=xgot.at[shift - 1, level, at],
             send_sem=xs.at[shift - 1], recv_sem=xr.at[i], device_id=peer, device_id_type=MESH)
 
     def rows_in(i):
@@ -391,13 +398,19 @@
             src_ref=ref, dst_ref=ref, send_sem=semaphore, recv_sem=fr.at[0, 0],
             device_id=peer_y(1), device_id_type=MESH).wait_send()
 
+    for shift in range(1, n_gx):
+        stage(shift).start()
     for turn_at in range(nblk):
         load(turn_at).start()
 
     pl.semaphore_wait(barrier, n_gx - 1 + above.astype(jnp.int32) + below.astype(jnp.int32))
 
     def send_ahead():
-        @pl.loop(0, depth)
+        for shift in range(1, n_gx):
+            stage(shift).wait()
+            rows_x(shift, 0, staged.at[shift - 1]).start()
+
+        @pl.loop(1, depth)
         def _(i):
             for shift in range(1, n_gx):
                 rows_x(shift, i).start()
@@ -638,6 +651,7 @@
             out_specs=(vmem, vmem),
             scratch_shapes=[
                 pltpu.VMEM((share, rows, cols), bf16),
+                pltpu.VMEM((xs, ROWS, cols), bf16),
                 pltpu.VMEM((xs, share, rows, cols), bf16),
                 pltpu.VMEM((peers + 1, chunks, bands, ROWS), bf16),
                 pltpu.VMEM((peers, chunks, bands, ROWS), bf16),
@@ -650,7 +664,7 @@
                 pltpu.VMEM((share * 16, size), f32),
                 pltpu.VMEM((peers + 1, 2 * share, bands), f32),
                 pltpu.VMEM((2, n_gx, 2 * share, bands), f32),
-                dma((nblk,)), dma((xs,)), dma((chunks,)), dma, dma((chunks,)),
+                dma((xs,)), dma((nblk,)), dma((xs,)), dma((chunks,)), dma, dma((chunks,)),
                 dma, dma((2, n_gx)), pltpu.SemaphoreType.REGULAR((3,)),
             ],
             compiler_params=pltpu.CompilerParams(

time: 117 us -> 117 us (level)
  no operation moved by 1% of the time
where the time goes in v5:
time: 117 us; the launch traced here: 116 us
  Pallas kernels  115 us (98%)
    pallas_call x1, Pallas kernels, body(): pl.pallas_call(functools.partial(fused_kernel, n_gx, n_gy, depth=DEPTH, l...  111 us
    pallas_call x1, Pallas kernels, body(): pl.pallas_call(store_kernel, out_shape=(jax.ShapeDtypeStruct((bands * lev...  3.73 us

profile of v5, /device:TPU:0, one launch (start us, length us, event | category | flops | bytes accessed | tf_op | source)
XLA Modules:
  0.0 115.6 jit_solution(7614255865141306317)
XLA Ops:
  0.6 111.2 %shard_map.30 = (f32[12,1536,128]{2,1,0:T(8,128)S(1)}, f32[11,8,192]{2,1,0:T(8,128)S(1)}) custom-call(bf16[8,384,768]{2,1,0:T(8,128)(2,1)} %field_ref.1), custom_call_target="tpu_custom_call" | custom-call | tf_op jit(solution)/shard_map/pallas_call | solution.py:644
  111.8 3.7 %shard_map.31 = (f32[1536,1536]{1,0:T(8,128)}, f32[11,8,192]{2,1,0:T(8,128)}) custom-call(f32[12,1536,128]{2,1,0:T(8,128)S(1)} %get-tuple-element.6.tile_ref, f32[11,8,192]{2,1,0:T(8,128)S(1)} %get-tuple-element.7.zone_ref), custom_call_target="tpu_custom_call" | custom-call | tf_op jit(solution)/shard_map/pallas_call | solution.py:673

commit v6 on v5

--- a/solution.py
+++ b/solution.py
@@ -702,7 +702,7 @@
 VMEM_LIMIT_STORE = 16 * 2**20
 DEPTH = 3
 LAG_LEAD = 1
-LAG = 3
+LAG = 4
 VMEM_LIMIT = 36 * 2**20
 
 

time: 117 us -> 117 us (level)
  no operation moved by 1% of the time
where the time goes in v6:
time: 117 us; the launch traced here: 116 us
  Pallas kernels  115 us (98%)
    pallas_call x1, Pallas kernels, body(): pl.pallas_call(functools.partial(fused_kernel, n_gx, n_gy, depth=DEPTH, l...  111 us
    pallas_call x1, Pallas kernels, body(): pl.pallas_call(store_kernel, out_shape=(jax.ShapeDtypeStruct((bands * lev...  3.73 us

profile of v6, /device:TPU:0, one launch (start us, length us, event | category | flops | bytes accessed | tf_op | source)
XLA Modules:
  0.0 115.6 jit_solution(13024714183951981798)
XLA Ops:
  0.6 111.2 %shard_map.30 = (f32[12,1536,128]{2,1,0:T(8,128)S(1)}, f32[11,8,192]{2,1,0:T(8,128)S(1)}) custom-call(bf16[8,384,768]{2,1,0:T(8,128)(2,1)} %field_ref.1), custom_call_target="tpu_custom_call" | custom-call | tf_op jit(solution)/shard_map/pallas_call | solution.py:644
  111.8 3.7 %shard_map.31 = (f32[1536,1536]{1,0:T(8,128)}, f32[11,8,192]{2,1,0:T(8,128)}) custom-call(f32[12,1536,128]{2,1,0:T(8,128)S(1)} %get-tuple-element.6.tile_ref, f32[11,8,192]{2,1,0:T(8,128)S(1)} %get-tuple-element.7.zone_ref), custom_call_target="tpu_custom_call" | custom-call | tf_op jit(solution)/shard_map/pallas_call | solution.py:673
